TPU v7x, 32 devices: a whole 2x2x4 slice. The times are simulated.
32 devices in a mesh: rep: 4 (over y, core), tp: 8 (over z, x).
Axes of the slice: x: 2, y: 2, z: 4, core: 2. Of those that a mesh axis runs over, the one named last changes fastest.
Arguments:
- activations: bfloat16 [4, 2048, 4096], P('rep', 'tp'), may hold values from -6 to 6
- cotangent: bfloat16 [4, 2048, 8192], P('rep', None, 'tp'), may hold values from -0.13183594 to 0.13183594
- drift: bfloat16 [4, 4096, 8192], P('rep', None, 'tp'), may hold values from -8 to 8
- outer_weights: float32 [4096, 8192], P(('rep', 'tp')), may hold values from -6 to 6
- momentum: float32 [4096, 8192], P(('rep', 'tp')), may hold values from -6 to 6
Outputs:
- weights: bfloat16 [4096, 8192], P(None, 'tp')
- new_outer: float32 [4096, 8192], P(('rep', 'tp'))
- new_momentum: float32 [4096, 8192], P(('rep', 'tp'))
All inputs are finite; a program needn't handle non-finite values.
Results may differ from a plain program's by a relative error of at most 0.0085.
Values may be sent and summed in bfloat16 or wider, within the bound.
No kernel may reach another device: no remote copies, remote signals or barrier semaphores. Data moves between devices by JAX's collectives and lax.ppermute only.
A program may use at most 128 MiB of HBM per device.

v0:
```python
import jax
import jax.numpy as jnp
from jax import lax
from jax.sharding import PartitionSpec as P

outer_rate = 0.7
nesterov = 0.9


def on_device(activations, cotangent, drift, outer_weights, momentum):
    replicas = lax.axis_size("rep")
    cot_rows = cotangent[0]
    grad = jnp.einsum(
        "td,tf->df",
        lax.all_gather(activations, "tp", axis=1, tiled=True)[0],
        cot_rows,
        preferred_element_type=jnp.float32,
    )
    delta = lax.optimization_barrier((drift[0].astype(jnp.float32) + grad).astype(jnp.bfloat16))
    summed = lax.psum_scatter(
        delta.astype(jnp.float32).astype(jnp.bfloat16), "rep", scatter_dimension=0, tiled=True
    ).astype(jnp.float32)
    summed = lax.all_to_all(
        summed.astype(jnp.bfloat16), "tp", split_axis=0, concat_axis=1, tiled=True
    ).astype(summed.dtype)
    average = summed / replicas
    new_momentum = nesterov * momentum + average
    new_outer = outer_weights - outer_rate * (average + nesterov * new_momentum)
    rounded = new_outer.astype(jnp.bfloat16)
    spread = lax.all_to_all(rounded, "tp", split_axis=1, concat_axis=0, tiled=True)
    weights = lax.all_gather(spread, "rep", axis=0, tiled=True)
    return (weights, new_outer, new_momentum)


def solution(mesh):
    in_specs = (
        P("rep", "tp", None),
        P("rep", None, "tp"),
        P("rep", None, "tp"),
        P(("rep", "tp"), None),
        P(("rep", "tp"), None),
    )
    out_specs = (P(None, "tp"), P(("rep", "tp"), None), P(("rep", "tp"), None))
    return jax.shard_map(
        on_device, mesh=mesh, in_specs=in_specs, out_specs=out_specs, check_vma=False
    )
```

profile of v0, /device:TPU:0, one launch (start us, length us, event | category | flops | bytes accessed | tf_op | source)
XLA Modules:
  0.0 532.6 jit_solution(2489531201938662445)
XLA Ops:
  7.2 0.0 all-gather.3.cloned.1.call-start
  7.2 0.7 all-gather.3.cloned.1.call-update
  7.9 0.0 reduce-scatter.2.cloned.1.call-start
  7.9 232.2 %all-gather.3.cloned.1.call-done = bf16[1,2048,4096]{2,1,0:T(8,128)(2,1)} async-done(((bf16[1,256,4096]{2,1,0:T(8,128)(2,1)}), bf16[1,2048,4096]{2,1,0:T(8,128)(2,1)}) %all-gather.3.cloned.1.call-update) | async-done | bytes 16777232 | tf_op jit(solution)/shard_map/all_gather | solution.py:15
  240.1 25.8 %fusion = bf16[4096,1024]{1,0:T(8,128)(2,1)} fusion(bf16[1,4096,1024]{2,1,0:T(8,128)(2,1)} %param.7, bf16[1,2048,4096]{2,1,0:T(8,128)(2,1)} %all-gather.3.cloned.1.call-done, bf16[1,2048,1024]{2,1,0:T(8,128)(2,1)} %param.6), kind=kOutput, calls=%fused_computation.1 | convolution fusion | flops 17192452096 | bytes 37748736 | tf_op jit(solution)/shard_map/td,tf->df/dot_general | solution.py:13
  266.0 0.0 reduce-scatter.2.cloned.1.call-update
  266.0 69.8 %reduce-scatter.2.cloned.1.call-done = bf16[1024,1024]{1,0:T(8,128)(2,1)} async-done(((bf16[4096,1024]{1,0:T(8,128)(2,1)}), bf16[1024,1024]{1,0:T(8,128)(2,1)}) %reduce-scatter.2.cloned.1.call-update) | async-done | bytes 2097168 | tf_op jit(solution)/shard_map/reduce_scatter | solution.py:20
  335.7 5.5 %all-to-all-start = ((bf16[8,128,1024]{2,1,0:T(8,128)(2,1)}), bf16[8,128,1024]{2,1,0:T(8,128)(2,1)S(1)}, u32[]{:S(2)}, u32[]{:S(2)}) async-start(bf16[8,128,1024]{2,1,0:T(8,128)(2,1)} %bitcast.30), calls=%async_computation.1 | async-start | bytes 4194304 | tf_op jit(solution)/shard_map/all_to_all | solution.py:23
  341.2 0.2 all-gather.5.cloned.1.call-start
  341.5 5.6 %copy.13 = f32[128,8192]{0,1:T(8,128)} copy(f32[128,8192]{1,0:T(8,128)} %param.8) | data formatting | bytes 8388608 | tf_op args[3]
  347.0 5.6 %copy.12 = f32[128,8192]{0,1:T(8,128)} copy(f32[128,8192]{1,0:T(8,128)} %param.9) | data formatting | bytes 8388608 | tf_op args[4]
  352.6 36.7 %all-to-all-done = bf16[8,128,1024]{2,1,0:T(8,128)(2,1)S(1)} async-done(((bf16[8,128,1024]{2,1,0:T(8,128)(2,1)}), bf16[8,128,1024]{2,1,0:T(8,128)(2,1)S(1)}, u32[]{:S(2)}, u32[]{:S(2)}) %all-to-all-start) | async-done | bytes 2097184 | tf_op jit(solution)/shard_map/all_to_all | solution.py:23
  389.3 2.6 multiply_bitcast_fusion
  391.9 5.3 %copy.11 = f32[128,8,1024]{0,2,1:T(8,128)} copy(f32[128,8,1024]{2,0,1:T(8,128)} %multiply_bitcast_fusion) | data formatting | bytes 8388608 | tf_op jit(solution)/shard_map/div | solution.py:26
  397.3 9.7 %fusion.8 = (bf16[128,8192]{0,1:T(8,128)(2,1)}, f32[128,8192]{0,1:T(8,128)}, f32[128,8192]{0,1:T(8,128)}) fusion(f32[128,8192]{0,1:T(8,128)} %copy.13, f32[128,8192]{0,1:T(8,128)} %copy.12, f32[128,8,1024]{0,2,1:T(8,128)} %copy.11), kind=kLoop, calls=%fused_computation.10 | loop fusion | flops 7340032 | bytes 23068672 | tf_op jit(solution)/shard_map/convert_element_type | solution.py:29
  406.9 2.9 copy.14
  409.8 51.9 %all_to_all.32 = bf16[128,8,1024]{2,0,1:T(8,128)(2,1)} all-to-all(bf16[128,8,1024]{2,0,1:T(8,128)(2,1)S(1)} %copy.14), channel_id=1, replica_groups=mesh['rep'=4,'tp'=8] {'tp'}, dimensions={1} | all-to-all | bytes 4194304 | tf_op jit(solution)/shard_map/all_to_all | solution.py:30
  461.7 0.0 all-gather.5.cloned.1.call-update
  461.7 5.6 %copy.15 = f32[128,8192]{1,0:T(8,128)} copy(f32[128,8192]{0,1:T(8,128)} %get-tuple-element.7) | data formatting | bytes 8388608
  467.4 6.0 %copy.16 = f32[128,8192]{1,0:T(8,128)} copy(f32[128,8192]{0,1:T(8,128)} %get-tuple-element.8) | data formatting | bytes 8388608
  473.3 45.0 %all-gather.5.cloned.1.call-done = bf16[4096,1024]{1,0:T(8,128)(2,1)} async-done(((bf16[1024,1024]{1,0:T(8,128)(2,1)}), bf16[4096,1024]{1,0:T(8,128)(2,1)}) %all-gather.5.cloned.1.call-update) | async-done | bytes 8388624 | tf_op jit(solution)/shard_map/all_gather | solution.py:31
  518.3 7.8 %copy.18 = bf16[4096,1024]{1,0:T(8,128)(2,1)} copy(bf16[4096,1024]{1,0:T(8,128)(2,1)} %all-gather.5.cloned.1.call-done) | data formatting | bytes 16777216
Async XLA Ops:
  7.2 233.0 %all-gather.3.cloned.1.call-start = ((), (), s32[]{:S(2)}) async-start(), calls=%async_computation.3 | async-start | bytes 18874368 | tf_op jit(solution)/shard_map/all_gather | solution.py:15
  7.9 327.8 %reduce-scatter.2.cloned.1.call-start = ((), (), s32[]{:S(2)}) async-start(), calls=%async_computation.4 | async-start | bytes 10485760 | tf_op jit(solution)/shard_map/reduce_scatter | solution.py:20
  335.7 53.6 %all-to-all-start = ((bf16[8,128,1024]{2,1,0:T(8,128)(2,1)}), bf16[8,128,1024]{2,1,0:T(8,128)(2,1)S(1)}, u32[]{:S(2)}, u32[]{:S(2)}) async-start(bf16[8,128,1024]{2,1,0:T(8,128)(2,1)} %bitcast.30), calls=%async_computation.1 | async-start | bytes 4194304 | tf_op jit(solution)/shard_map/all_to_all | solution.py:23
  341.2 177.0 %all-gather.5.cloned.1.call-start = ((), (), s32[]{:S(2)}) async-start(), calls=%async_computation.5 | async-start | bytes 10485760 | tf_op jit(solution)/shard_map/all_gather | solution.py:31
Sparse Core Ops, SparseCore 0:
  10.1 229.9 all-gather.2
  266.1 69.5 reduce-scatter.1
  461.9 56.3 all-gather.4
where the time goes:
time: 533 us
  waiting for transfers between devices  384 us (72%)
  blocking collectives  51.9 us (10%)
  local copies, waits for them, and re-layouts  38.6 us (7%)
  matrix products  25.8 us (5%)
  between operations  13.8 us (3%)
  other arithmetic  12.3 us (2%)
  starting transfers between devices  5.8 us (1%)
    all_gather x1, waiting for transfers between devices, on_device(): lax.all_gather(activations, 'tp', axis=1, tiled=True)[0]  232 us
    reduce_scatter x1, waiting for transfers between devices, on_device(): lax.psum_scatter(delta.astype(jnp.float32).astype(jnp.bfloat16), 'rep', s...  69.8 us
    all_to_all x1, blocking collectives, on_device(): lax.all_to_all(rounded, 'tp', split_axis=1, concat_axis=0, tiled=True)  51.9 us
    all_gather x1, waiting for transfers between devices, on_device(): weights = lax.all_gather(spread, 'rep', axis=0, tiled=True)  45 us
    all_to_all x1, waiting for transfers between devices, on_device(): lax.all_to_all(summed.astype(jnp.bfloat16), 'tp', split_axis=0, concat_ax...  36.7 us
    unnamed x5, local copies, waits for them, and re-layouts  30.5 us
    dot_general x1, matrix products, on_device(): jnp.einsum('td,tf->df', lax.all_gather(activations, 'tp', axis=1, tiled=T...  25.8 us
  transfers between devices with their start and end apart: 4, of which 4 were waited for; matrix products, arithmetic and copies ran while one was open for 4% of the time, Pallas kernels for 0%

commit v1 on v0

--- a/solution.py
+++ b/solution.py
@@ -20,8 +20,14 @@
     summed = lax.psum_scatter(
         delta.astype(jnp.float32).astype(jnp.bfloat16), "rep", scatter_dimension=0, tiled=True
     ).astype(jnp.float32)
-    summed = lax.all_to_all(
-        summed.astype(jnp.bfloat16), "tp", split_axis=0, concat_axis=1, tiled=True
+    summed = jnp.concatenate(
+        lax.all_to_all(
+            jnp.stack(jnp.split(summed.astype(jnp.bfloat16), lax.axis_size("tp"), axis=0)),
+            "tp",
+            0,
+            0,
+        ),
+        axis=1,
     ).astype(summed.dtype)
     average = summed / replicas
     new_momentum = nesterov * momentum + average

time: 533 us -> 546 us (1.024)
  local copies, waits for them, and re-layouts: 38.6 us -> 51.8 us
    unnamed x5 -> x12, local copies, waits for them, and re-layouts: 30.5 us -> 42.1 us
where the time goes in v1:
time: 546 us; the launch traced here: 545 us
  waiting for transfers between devices  385 us (71%)
  local copies, waits for them, and re-layouts  51.8 us (9%)
  blocking collectives  51.8 us (9%)
  matrix products  25.8 us (5%)
  between operations  13.8 us (3%)
  other arithmetic  11.8 us (2%)
  starting transfers between devices  5.61 us (1%)
    all_gather x1, waiting for transfers between devices, on_device(): lax.all_gather(activations, 'tp', axis=1, tiled=True)[0]  232 us
    reduce_scatter x1, waiting for transfers between devices, on_device(): lax.psum_scatter(delta.astype(jnp.float32).astype(jnp.bfloat16), 'rep', s...  69.8 us
    all_to_all x1, blocking collectives, on_device(): lax.all_to_all(rounded, 'tp', split_axis=1, concat_axis=0, tiled=True)  51.8 us
    all_gather x1, waiting for transfers between devices, on_device(): weights = lax.all_gather(spread, 'rep', axis=0, tiled=True)  45 us
    unnamed x12, local copies, waits for them, and re-layouts  42.1 us
    all_to_all x1, waiting for transfers between devices, on_device(): lax.all_to_all(jnp.stack(jnp.split(summed.astype(jnp.bfloat16), lax.axis_...  36.9 us
    dot_general x1, matrix products, on_device(): jnp.einsum('td,tf->df', lax.all_gather(activations, 'tp', axis=1, tiled=T...  25.8 us
  transfers between devices with their start and end apart: 4, of which 4 were waited for; matrix products, arithmetic and copies ran while one was open for 4% of the time, Pallas kernels for 0%

profile of v1, /device:TPU:0, one launch (start us, length us, event | category | flops | bytes accessed | tf_op | source)
XLA Modules:
  0.0 545.1 jit_solution(16707470038937861957)
XLA Ops:
  7.2 0.0 all-gather.3.cloned.1.call-start
  7.2 0.7 all-gather.3.cloned.1.call-update
  7.9 0.0 reduce-scatter.2.cloned.1.call-start
  7.9 232.2 %all-gather.3.cloned.1.call-done = bf16[1,2048,4096]{2,1,0:T(8,128)(2,1)} async-done(((bf16[1,256,4096]{2,1,0:T(8,128)(2,1)}), bf16[1,2048,4096]{2,1,0:T(8,128)(2,1)}) %all-gather.3.cloned.1.call-update) | async-done | bytes 16777232 | tf_op jit(solution)/shard_map/all_gather | solution.py:15
  240.1 25.8 %fusion = bf16[4096,1024]{1,0:T(8,128)(2,1)} fusion(bf16[1,4096,1024]{2,1,0:T(8,128)(2,1)} %param.7, bf16[1,2048,4096]{2,1,0:T(8,128)(2,1)} %all-gather.3.cloned.1.call-done, bf16[1,2048,1024]{2,1,0:T(8,128)(2,1)} %param.6), kind=kOutput, calls=%fused_computation.1 | convolution fusion | flops 17192452096 | bytes 37748736 | tf_op jit(solution)/shard_map/td,tf->df/dot_general | solution.py:13
  266.0 0.0 reduce-scatter.2.cloned.1.call-update
  266.0 69.8 %reduce-scatter.2.cloned.1.call-done = bf16[1024,1024]{1,0:T(8,128)(2,1)} async-done(((bf16[4096,1024]{1,0:T(8,128)(2,1)}), bf16[1024,1024]{1,0:T(8,128)(2,1)}) %reduce-scatter.2.cloned.1.call-update) | async-done | bytes 2097168 | tf_op jit(solution)/shard_map/reduce_scatter | solution.py:20
  335.7 1.7 fusion.15
  337.4 1.7 fusion.14
  339.1 1.7 fusion.13
  340.8 1.7 fusion.12
  342.4 1.7 fusion.11
  344.1 1.7 fusion.10
  345.8 1.7 fusion.9
  347.4 1.7 fusion.8
  349.1 5.5 %all-to-all-start = ((bf16[8,128,1024]{2,1,0:T(8,128)(2,1)}), bf16[8,128,1024]{2,1,0:T(8,128)(2,1)S(1)}, u32[]{:S(2)}, u32[]{:S(2)}) async-start(bf16[8,128,1024]{2,1,0:T(8,128)(2,1)} %fusion.8), calls=%async_computation.1 | async-start | bytes 4194304 | tf_op jit(solution)/shard_map/all_to_all | solution.py:24
  354.6 0.0 all-gather.5.cloned.1.call-start
  354.6 5.6 %copy.11 = f32[128,8192]{0,1:T(8,128)} copy(f32[128,8192]{1,0:T(8,128)} %param.8) | data formatting | bytes 8388608 | tf_op args[3]
  360.2 5.6 %copy.10 = f32[128,8192]{0,1:T(8,128)} copy(f32[128,8192]{1,0:T(8,128)} %param.9) | data formatting | bytes 8388608 | tf_op args[4]
  365.8 36.9 %all-to-all-done = bf16[8,128,1024]{2,1,0:T(8,128)(2,1)S(1)} async-done(((bf16[8,128,1024]{2,1,0:T(8,128)(2,1)}), bf16[8,128,1024]{2,1,0:T(8,128)(2,1)S(1)}, u32[]{:S(2)}, u32[]{:S(2)}) %all-to-all-start) | async-done | bytes 2097184 | tf_op jit(solution)/shard_map/all_to_all | solution.py:24
  402.7 2.6 multiply_bitcast_fusion
  405.3 5.3 copy.9
  410.6 9.2 %fusion.16 = (bf16[128,8192]{0,1:T(8,128)(2,1)S(1)}, f32[128,8192]{0,1:T(8,128)}, f32[128,8192]{0,1:T(8,128)}) fusion(f32[128,8192]{0,1:T(8,128)} %copy.11, f32[128,8192]{0,1:T(8,128)} %copy.10, f32[128,8,1024]{0,2,1:T(8,128)} %copy.9), kind=kLoop, calls=%fused_computation.26 | loop fusion | flops 7340032 | bytes 23068672 | tf_op jit(solution)/shard_map/convert_element_type | solution.py:35
  419.8 51.8 %all_to_all.24 = bf16[128,8,1024]{0,2,1:T(8,128)(2,1)S(1)} all-to-all(bf16[128,8,1024]{0,2,1:T(8,128)(2,1)S(1)} %bitcast.60), channel_id=1, replica_groups=mesh['rep'=4,'tp'=8] {'tp'}, dimensions={1} | all-to-all | bytes 4194304 | tf_op jit(solution)/shard_map/all_to_all | solution.py:36
  471.6 2.6 copy.12
  474.3 0.0 all-gather.5.cloned.1.call-update
  474.3 5.6 %copy.13 = f32[128,8192]{1,0:T(8,128)} copy(f32[128,8192]{0,1:T(8,128)} %get-tuple-element.7) | data formatting | bytes 8388608
  479.9 6.0 %copy.14 = f32[128,8192]{1,0:T(8,128)} copy(f32[128,8192]{0,1:T(8,128)} %get-tuple-element.8) | data formatting | bytes 8388608
  485.9 45.0 %all-gather.5.cloned.1.call-done = bf16[4096,1024]{1,0:T(8,128)(2,1)} async-done(((bf16[1024,1024]{1,0:T(8,128)(2,1)}), bf16[4096,1024]{1,0:T(8,128)(2,1)}) %all-gather.5.cloned.1.call-update) | async-done | bytes 8388624 | tf_op jit(solution)/shard_map/all_gather | solution.py:37
  530.8 7.8 %copy.23 = bf16[4096,1024]{1,0:T(8,128)(2,1)} copy(bf16[4096,1024]{1,0:T(8,128)(2,1)} %all-gather.5.cloned.1.call-done) | data formatting | bytes 16777216
Async XLA Ops:
  7.2 233.0 %all-gather.3.cloned.1.call-start = ((), (), s32[]{:S(2)}) async-start(), calls=%async_computation.3 | async-start | bytes 18874368 | tf_op jit(solution)/shard_map/all_gather | solution.py:15
  7.9 327.8 %reduce-scatter.2.cloned.1.call-start = ((), (), s32[]{:S(2)}) async-start(), calls=%async_computation.4 | async-start | bytes 10485760 | tf_op jit(solution)/shard_map/reduce_scatter | solution.py:20
  349.1 53.6 %all-to-all-start = ((bf16[8,128,1024]{2,1,0:T(8,128)(2,1)}), bf16[8,128,1024]{2,1,0:T(8,128)(2,1)S(1)}, u32[]{:S(2)}, u32[]{:S(2)}) async-start(bf16[8,128,1024]{2,1,0:T(8,128)(2,1)} %fusion.8), calls=%async_computation.1 | async-start | bytes 4194304 | tf_op jit(solution)/shard_map/all_to_all | solution.py:24
  354.6 176.2 %all-gather.5.cloned.1.call-start = ((), (), s32[]{:S(2)}) async-start(), calls=%async_computation.5 | async-start | bytes 10485760 | tf_op jit(solution)/shard_map/all_gather | solution.py:37
Sparse Core Ops, SparseCore 0:
  10.1 229.9 all-gather.2
  266.1 69.5 reduce-scatter.1
  474.4 56.3 all-gather.4

commit v2 on v0

--- a/solution.py
+++ b/solution.py
@@ -28,7 +28,12 @@
     new_outer = outer_weights - outer_rate * (average + nesterov * new_momentum)
     rounded = new_outer.astype(jnp.bfloat16)
     spread = lax.all_to_all(rounded, "tp", split_axis=1, concat_axis=0, tiled=True)
-    weights = lax.all_gather(spread, "rep", axis=0, tiled=True)
+    ring = [spread]
+    for hop in range(3):
+        ring.append(lax.ppermute(ring[-1], "rep", [(dev, (dev + 1) % 4) for dev in range(4)]))
+    weights = jnp.roll(
+        jnp.concatenate(ring[::-1], axis=0), (lax.axis_index("rep") + 1) * ring[0].shape[0], axis=0
+    )
     return (weights, new_outer, new_momentum)
 
 

time: 533 us -> 573 us (1.075)
  waiting for transfers between devices: 384 us -> 405 us
  local copies, waits for them, and re-layouts: 38.6 us -> 57.7 us
    ppermute x0 -> x3, waiting for transfers between devices: none -> 65.6 us  [on_device(): lax.ppermute(ring[-1], 'rep', [(dev, (dev + 1) % 4) for dev in range(4)])]
    all_gather x1 -> x0, waiting for transfers between devices: 45 us -> none  [on_device(): weights = lax.all_gather(spread, 'rep', axis=0, tiled=True)]
    unnamed x5 -> x15, local copies, waits for them, and re-layouts: 30.5 us -> 40.5 us
    dynamic_slice x0 -> x1, local copies, waits for them, and re-layouts: none -> 7.76 us  [on_device(): jnp.roll(jnp.concatenate(ring[::-1], axis=0), (lax.axis_index('rep') + 1)...]
  transfers between devices with their start and end apart: 4 -> 6, of which waited for: 4 -> 6; matrix products, arithmetic and copies ran while one was open for 4% -> 4% of each run, Pallas kernels for 0% -> 0%
where the time goes in v2:
time: 573 us; the launch traced here: 572 us
  waiting for transfers between devices  405 us (71%)
  local copies, waits for them, and re-layouts  57.7 us (10%)
  blocking collectives  52 us (9%)
  matrix products  25.8 us (5%)
  between operations  14.1 us (2%)
  other arithmetic  11.8 us (2%)
    all_gather x1, waiting for transfers between devices, on_device(): lax.all_gather(activations, 'tp', axis=1, tiled=True)[0]  232 us
    reduce_scatter x1, waiting for transfers between devices, on_device(): lax.psum_scatter(delta.astype(jnp.float32).astype(jnp.bfloat16), 'rep', s...  69.8 us
    ppermute x3, waiting for transfers between devices, on_device(): lax.ppermute(ring[-1], 'rep', [(dev, (dev + 1) % 4) for dev in range(4)])  65.6 us
    all_to_all x1, blocking collectives, on_device(): lax.all_to_all(rounded, 'tp', split_axis=1, concat_axis=0, tiled=True)  52 us
    unnamed x15, local copies, waits for them, and re-layouts  40.5 us
    all_to_all x1, waiting for transfers between devices, on_device(): lax.all_to_all(summed.astype(jnp.bfloat16), 'tp', split_axis=0, concat_ax...  36.9 us
    dot_general x1, matrix products, on_device(): jnp.einsum('td,tf->df', lax.all_gather(activations, 'tp', axis=1, tiled=T...  25.8 us
  transfers between devices with their start and end apart: 6, of which 6 were waited for; matrix products, arithmetic and copies ran while one was open for 4% of the time, Pallas kernels for 0%

profile of v2, /device:TPU:0, one launch (start us, length us, event | category | flops | bytes accessed | tf_op | source)
XLA Modules:
  0.0 572.2 jit_solution(15292368327214790420)
XLA Ops:
  7.2 0.0 all-gather.2.cloned.1.call-start
  7.2 0.7 all-gather.2.cloned.1.call-update
  7.9 0.0 reduce-scatter.2.cloned.1.call-start
  7.9 232.2 %all-gather.2.cloned.1.call-done = bf16[1,2048,4096]{2,1,0:T(8,128)(2,1)} async-done(((bf16[1,256,4096]{2,1,0:T(8,128)(2,1)}), bf16[1,2048,4096]{2,1,0:T(8,128)(2,1)}) %all-gather.2.cloned.1.call-update) | async-done | bytes 16777232 | tf_op jit(solution)/shard_map/all_gather | solution.py:15
  240.1 25.8 %fusion = bf16[4096,1024]{1,0:T(8,128)(2,1)} fusion(bf16[1,4096,1024]{2,1,0:T(8,128)(2,1)} %param.7, bf16[1,2048,4096]{2,1,0:T(8,128)(2,1)} %all-gather.2.cloned.1.call-done, bf16[1,2048,1024]{2,1,0:T(8,128)(2,1)} %param.6), kind=kOutput, calls=%fused_computation.1 | convolution fusion | flops 17192452096 | bytes 37748736 | tf_op jit(solution)/shard_map/td,tf->df/dot_general | solution.py:13
  266.0 0.0 reduce-scatter.2.cloned.1.call-update
  266.0 69.8 %reduce-scatter.2.cloned.1.call-done = bf16[1024,1024]{1,0:T(8,128)(2,1)} async-done(((bf16[4096,1024]{1,0:T(8,128)(2,1)}), bf16[1024,1024]{1,0:T(8,128)(2,1)}) %reduce-scatter.2.cloned.1.call-update) | async-done | bytes 2097168 | tf_op jit(solution)/shard_map/reduce_scatter | solution.py:20
  335.7 5.5 all-to-all-start
  341.2 5.6 copy.13
  346.8 5.6 copy.12
  352.4 36.9 %all-to-all-done = bf16[8,128,1024]{2,1,0:T(8,128)(2,1)S(1)} async-done(((bf16[8,128,1024]{2,1,0:T(8,128)(2,1)}), bf16[8,128,1024]{2,1,0:T(8,128)(2,1)S(1)}, u32[]{:S(2)}, u32[]{:S(2)}) %all-to-all-start) | async-done | bytes 2097184 | tf_op jit(solution)/shard_map/all_to_all | solution.py:23
  389.3 2.6 multiply_bitcast_fusion
  391.9 5.3 copy.11
  397.3 9.2 %fusion.8 = (bf16[128,8192]{0,1:T(8,128)(2,1)S(1)}, f32[128,8192]{0,1:T(8,128)}, f32[128,8192]{0,1:T(8,128)}) fusion(f32[128,8192]{0,1:T(8,128)} %copy.13, f32[128,8192]{0,1:T(8,128)} %copy.12, f32[128,8,1024]{0,2,1:T(8,128)} %copy.11), kind=kLoop, calls=%fused_computation.19 | loop fusion | flops 7340032 | bytes 23068672 | tf_op jit(solution)/shard_map/convert_element_type | solution.py:29
  406.5 2.6 copy.14
  409.1 52.0 %all_to_all.32 = bf16[128,8,1024]{2,0,1:T(8,128)(2,1)S(1)} all-to-all(bf16[128,8,1024]{2,0,1:T(8,128)(2,1)} %copy.14), channel_id=1, replica_groups=mesh['rep'=4,'tp'=8] {'tp'}, dimensions={1} | all-to-all | bytes 4194304 | tf_op jit(solution)/shard_map/all_to_all | solution.py:30
  461.1 0.0 collective-permute-start
  461.1 25.5 %collective-permute-done = bf16[1024,1024]{1,0:T(8,128)(2,1)S(1)} collective-permute-done((bf16[1024,1024]{1,0:T(8,128)(2,1)S(1)}, bf16[1024,1024]{1,0:T(8,128)(2,1)S(1)}, u32[]{:S(2)}, u32[]{:S(2)}) %collective-permute-start) | collective-permute-done | bytes 2097184 | tf_op jit(solution)/shard_map/ppermute | solution.py:33
  486.5 1.3 copy-done
  487.9 25.6 %collective-permute-done.1 = bf16[1024,1024]{1,0:T(8,128)(2,1)} collective-permute-done((bf16[1024,1024]{1,0:T(8,128)(2,1)S(1)}, bf16[1024,1024]{1,0:T(8,128)(2,1)}, u32[]{:S(2)}, u32[]{:S(2)}) %collective-permute-start.1) | collective-permute-done | bytes 2097184 | tf_op jit(solution)/shard_map/ppermute | solution.py:33
  513.4 5.6 copy.15
  519.0 5.6 copy.16
  524.6 14.6 %collective-permute-done.2 = bf16[1024,1024]{1,0:T(8,128)(2,1)} collective-permute-done((bf16[1024,1024]{1,0:T(8,128)(2,1)}, bf16[1024,1024]{1,0:T(8,128)(2,1)}, u32[]{:S(2)}, u32[]{:S(2)}) %collective-permute-start.2) | collective-permute-done | bytes 2097184 | tf_op jit(solution)/shard_map/ppermute | solution.py:33
  539.2 3.1 constant_dynamic-update-slice_fusion.7
  542.3 3.1 constant_dynamic-update-slice_fusion.6
  545.4 1.5 constant_dynamic-update-slice_fusion.5
  546.9 1.5 constant_dynamic-update-slice_fusion.4
  548.4 3.1 constant_dynamic-update-slice_fusion.3
  551.5 3.1 constant_dynamic-update-slice_fusion.2
  554.6 1.5 constant_dynamic-update-slice_fusion.1
  556.1 1.5 constant_dynamic-update-slice_fusion
  557.6 7.8 %constant_dynamic-slice_fusion = bf16[4096,1024]{1,0:T(8,128)(2,1)} fusion(bf16[8192,1024]{1,0:T(8,128)(2,1)} %constant_dynamic-update-slice_fusion, s32[]{:T(128)S(6)} %select_n.14), kind=kLoop, calls=%fused_computation.18 | loop fusion | bytes 16777220 | tf_op jit(solution)/shard_map/jit(_roll_dynamic)/dynamic_slice | solution.py:34
  (5 shorter events, 0.0 us)
Async XLA Ops:
  7.2 233.0 %all-gather.2.cloned.1.call-start = ((), (), s32[]{:S(2)}) async-start(), calls=%async_computation.3 | async-start | bytes 18874368 | tf_op jit(solution)/shard_map/all_gather | solution.py:15
  7.9 327.8 %reduce-scatter.2.cloned.1.call-start = ((), (), s32[]{:S(2)}) async-start(), calls=%async_computation.4 | async-start | bytes 10485760 | tf_op jit(solution)/shard_map/reduce_scatter | solution.py:20
  335.7 53.6 %all-to-all-start = ((bf16[8,128,1024]{2,1,0:T(8,128)(2,1)}), bf16[8,128,1024]{2,1,0:T(8,128)(2,1)S(1)}, u32[]{:S(2)}, u32[]{:S(2)}) async-start(bf16[8,128,1024]{2,1,0:T(8,128)(2,1)} %bitcast.32), calls=%async_computation.1 | async-start | bytes 4194304 | tf_op jit(solution)/shard_map/all_to_all | solution.py:23
  461.1 25.5 %collective-permute-start = (bf16[1024,1024]{1,0:T(8,128)(2,1)S(1)}, bf16[1024,1024]{1,0:T(8,128)(2,1)S(1)}, u32[]{:S(2)}, u32[]{:S(2)}) collective-permute-start(bf16[1024,1024]{1,0:T(8,128)(2,1)S(1)} %bitcast.28), channel_id=1, source_target_pairs={{0,8},{8,16},{16,24},{24,0},{1,9},{9,17},{17,25},{25,1},{2,10},{10... | collective-permute-start | bytes 6291464 | tf_op jit(solution)/shard_map/ppermute | solution.py:33
  486.5 1.3 copy-start
  487.9 25.6 %collective-permute-start.1 = (bf16[1024,1024]{1,0:T(8,128)(2,1)S(1)}, bf16[1024,1024]{1,0:T(8,128)(2,1)}, u32[]{:S(2)}, u32[]{:S(2)}) collective-permute-start(bf16[1024,1024]{1,0:T(8,128)(2,1)S(1)} %collective-permute-done), channel_id=1, source_target_pairs={{0,8},{8,16},{16,24},{24,0},{1,9},{9,17},{17,25},{25,1},{2,10},{10... | collective-permute-start | bytes 6291464 | tf_op jit(solution)/shard_map/ppermute | solution.py:33
  513.4 25.8 %collective-permute-start.2 = (bf16[1024,1024]{1,0:T(8,128)(2,1)}, bf16[1024,1024]{1,0:T(8,128)(2,1)}, u32[]{:S(2)}, u32[]{:S(2)}) collective-permute-start(bf16[1024,1024]{1,0:T(8,128)(2,1)} %collective-permute-done.1), channel_id=1, source_target_pairs={{0,8},{8,16},{16,24},{24,0},{1,9},{9,17},{17,25},{25,1},{2,10},{10... | collective-permute-start | bytes 6291464 | tf_op jit(solution)/shard_map/ppermute | solution.py:33
  524.6 20.8 %copy-start.1 = (bf16[1024,1024]{1,0:T(8,128)(2,1)S(1)}, bf16[1024,1024]{1,0:T(8,128)(2,1)}, u32[]{:S(2)}) copy-start(bf16[1024,1024]{1,0:T(8,128)(2,1)} %copy-done) | copy-start | bytes 6291460
Sparse Core Ops, SparseCore 0:
  10.1 229.9 all-gather.1
  266.1 69.5 reduce-scatter.1
